TPU v7x, 32 devices: a whole 2x2x4 slice. The times are simulated.
32 devices in a mesh: ctx: 8 (over z, x), fsdp: 4 (over y, core).
Axes of the slice: x: 2, y: 2, z: 4, core: 2. Of those that a mesh axis runs over, the one named last changes fastest.
Arguments:
- tokens: bfloat16 [4, 1024, 1600], P('fsdp', 'ctx'), may hold values from -40 to 40, as said below
- ln1_gain: bfloat16 [1600], P('fsdp'), may hold values from 0.099609375 to 1.8984375
- ln1_shift: bfloat16 [1600], P('fsdp'), may hold values from -3 to 3
- qkv_weight: bfloat16 [1600, 4800], P('fsdp'), may hold values from -0.15625 to 0.15625
- qv_bias: bfloat16 [3200], P('fsdp'), may hold values from -3 to 3
- out_weight: bfloat16 [1600, 1600], P('fsdp'), may hold values from -1.25 to 1.25
- out_bias: bfloat16 [1600], P('fsdp'), may hold values from -3 to 3
- ln2_gain: bfloat16 [1600], P('fsdp'), may hold values from 0.099609375 to 1.8984375
- ln2_shift: bfloat16 [1600], P('fsdp'), may hold values from -3 to 3
- up_weight: bfloat16 [1600, 6400], P('fsdp'), may hold values from -0.15625 to 0.15625
- up_bias: bfloat16 [6400], P('fsdp'), may hold values from -3 to 3
- down_weight: bfloat16 [6400, 1600], P('fsdp'), may hold values from -0.078125 to 0.078125
- down_bias: bfloat16 [1600], P('fsdp'), may hold values from -3 to 3
- block_table: int32 [8], replicated, may hold values from 0 to 7, each once
- cotangent: bfloat16 [4, 1024, 1600], P('fsdp', 'ctx'), may hold values from -6 to 6
Outputs:
- block_out: float32 [4, 1024, 1600], P('fsdp', 'ctx')
- input_grad: float32 [4, 1024, 1600], P('fsdp', 'ctx')
- ln1_gain_grad: float32 [1600], P('fsdp')
- ln1_shift_grad: float32 [1600], P('fsdp')
- qkv_weight_grad: float32 [1600, 4800], P('fsdp')
- qv_bias_grad: float32 [3200], P('fsdp')
- out_weight_grad: float32 [1600, 1600], P('fsdp')
- out_bias_grad: float32 [1600], P('fsdp')
- ln2_gain_grad: float32 [1600], P('fsdp')
- ln2_shift_grad: float32 [1600], P('fsdp')
- up_weight_grad: float32 [1600, 6400], P('fsdp')
- up_bias_grad: float32 [6400], P('fsdp')
- down_weight_grad: float32 [6400, 1600], P('fsdp')
- down_bias_grad: float32 [1600], P('fsdp')
Inputs may be any that keep to these rules, and one draw needn't show every extreme that they name: Device c of ctx holds blocks block_table[c] and 15 - block_table[c] of each of its sequence, in that order; every value appears once. `tokens`: activations of order one.
All inputs are finite; a program needn't handle non-finite values.
Results may differ from a plain program's by a relative error of at most 0.017.
Values may be sent and summed in bfloat16 or wider, within the bound.
A program may use at most 384 MiB of HBM per device.

v0:
```python
import jax
import jax.numpy as jnp
from jax import lax
from jax.sharding import PartitionSpec as P

HEAD_DIM = 64
EPS = 1e-05
SCALE = 0.125


def layer_norm(value, gain, shift):
    centre = value - jnp.mean(value, axis=-1, keepdims=True)
    spread = jnp.mean(centre * centre, axis=-1, keepdims=True)
    return centre * lax.rsqrt(spread + EPS) * gain + shift


def gelu_tanh(value):
    return jax.nn.gelu(value, approximate=True)


def inner_rows(left, right):
    return lax.dot_general(
        left, right, (((0,), (0,)), ((), ())), preferred_element_type=jnp.float32
    )


def times_transpose(left, right):
    return lax.dot_general(
        left, right, (((1,), (1,)), ((), ())), preferred_element_type=jnp.float32
    )


def exponents(query_part, query_place, key_part, key_place):
    raw = jnp.einsum("qhd,khd->hqk", query_part, key_part, preferred_element_type=jnp.float32)
    allowed = key_place[None, None, :] <= query_place[None, :, None]
    return jnp.where(allowed, jnp.exp(raw * SCALE), 0.0)


def score_grads(
    query_part, scaled_part, correction_part, query_place, key_part, value_part, key_place
):
    exponent = exponents(query_part, query_place, key_part, key_place)
    d_expo = jnp.einsum("qhd,khd->hqk", scaled_part, value_part, preferred_element_type=jnp.float32)
    d_raw = (exponent * (d_expo - correction_part.T[:, :, None])).astype(jnp.bfloat16) * SCALE
    return (exponent, d_raw)


def on_device(
    tokens,
    ln1_gain,
    ln1_shift,
    qkv_weight,
    qv_bias,
    out_weight,
    out_bias,
    ln2_gain,
    ln2_shift,
    up_weight,
    up_bias,
    down_weight,
    down_bias,
    block_table,
    cotangent,
):
    rows = tokens.shape[1]
    width = tokens.shape[2]
    heads = width // HEAD_DIM
    half = rows // 2
    count = lax.axis_size("ctx")
    within = jnp.arange(rows, dtype=jnp.int32)
    block_of = jnp.where(
        within[None, :] < half, block_table[:, None], 2 * count - 1 - block_table[:, None]
    )
    place = block_of * half + within[None, :] % half
    device = lax.axis_index("ctx")
    query_place = jnp.sum(
        jnp.where(jnp.arange(count, dtype=jnp.int32)[:, None] == device, place, 0), axis=0
    )
    key_place = place.reshape(-1)
    kblock = 4 * rows
    nblock = key_place.shape[0] // kblock
    place_blocks = key_place.reshape(nblock, kblock)
    attn_parts = (
        lax.all_gather(ln1_gain, "fsdp", axis=0, tiled=True),
        lax.all_gather(ln1_shift, "fsdp", axis=0, tiled=True),
        lax.all_gather(qkv_weight, "fsdp", axis=0, tiled=True),
        lax.all_gather(qv_bias, "fsdp", axis=0, tiled=True),
        lax.all_gather(out_weight, "fsdp", axis=0, tiled=True),
        lax.all_gather(out_bias, "fsdp", axis=0, tiled=True),
    )
    gain1 = attn_parts[0].astype(jnp.float32)
    shift1 = attn_parts[1].astype(jnp.float32)
    w_qkv = attn_parts[2]
    b_qv = attn_parts[3].astype(jnp.float32)
    w_out = attn_parts[4]
    b_out = attn_parts[5].astype(jnp.float32)
    inputs = tokens[0].astype(jnp.float32)
    normed1, ln1_back = jax.vjp(layer_norm, inputs, gain1, shift1)
    act1 = normed1.astype(jnp.bfloat16)
    projected = jnp.dot(act1, w_qkv, preferred_element_type=jnp.float32)
    query = (projected[:, :width] + b_qv[:width]).astype(jnp.bfloat16)
    keys = projected[:, width : 2 * width].astype(jnp.bfloat16)
    values = (projected[:, 2 * width :] + b_qv[width:]).astype(jnp.bfloat16)
    keys_all, values_all = (
        lax.all_gather(keys, "ctx", axis=0, tiled=True),
        lax.all_gather(values, "ctx", axis=0, tiled=True),
    )
    key_blocks = keys_all.reshape(nblock, kblock, heads, HEAD_DIM)
    value_blocks = values_all.reshape(nblock, kblock, heads, HEAD_DIM)
    query3 = query.reshape(rows, heads, HEAD_DIM)

    def forward_step(carry, parts):
        total, numerator = carry
        key_part, value_part, part_place = parts
        exponent = exponents(query3, query_place, key_part, part_place)
        total = total + jnp.sum(exponent, axis=2)
        numerator = numerator + jnp.einsum(
            "hqk,khd->qhd",
            exponent.astype(jnp.bfloat16),
            value_part,
            preferred_element_type=jnp.float32,
        )
        return ((total, numerator), None)

    begin = (jnp.zeros((heads, rows), jnp.float32), jnp.zeros((rows, heads, HEAD_DIM), jnp.float32))
    (total, numerator), _ = lax.scan(forward_step, begin, (key_blocks, value_blocks, place_blocks))
    totals_rows = total.T
    attended = numerator / totals_rows[:, :, None]
    attn = attended.reshape(rows, width).astype(jnp.bfloat16)
    mid = inputs + jnp.dot(attn, w_out, preferred_element_type=jnp.float32) + b_out
    mlp_parts = (
        lax.all_gather(ln2_gain, "fsdp", axis=0, tiled=True),
        lax.all_gather(ln2_shift, "fsdp", axis=0, tiled=True),
        lax.all_gather(up_weight, "fsdp", axis=0, tiled=True),
        lax.all_gather(up_bias, "fsdp", axis=0, tiled=True),
        lax.all_gather(down_weight, "fsdp", axis=0, tiled=True),
        lax.all_gather(down_bias, "fsdp", axis=0, tiled=True),
    )
    gain2 = mlp_parts[0].astype(jnp.float32)
    shift2 = mlp_parts[1].astype(jnp.float32)
    w_up = mlp_parts[2]
    b_up = mlp_parts[3].astype(jnp.float32)
    w_down = mlp_parts[4]
    b_down = mlp_parts[5].astype(jnp.float32)
    normed2, ln2_back = jax.vjp(layer_norm, mid, gain2, shift2)
    act2 = normed2.astype(jnp.bfloat16)
    hidden_in = jnp.dot(act2, w_up, preferred_element_type=jnp.float32) + b_up
    activated, gelu_back = jax.vjp(gelu_tanh, hidden_in)
    hidden = activated.astype(jnp.bfloat16)
    result = mid + jnp.dot(hidden, w_down, preferred_element_type=jnp.float32) + b_down
    grad_out = cotangent[0].astype(jnp.float32)
    grad_branch2 = grad_out.astype(jnp.bfloat16)
    d_down = inner_rows(hidden, grad_branch2)
    d_down_bias = jnp.sum(grad_branch2.astype(jnp.float32), axis=0)
    d_hidden = times_transpose(grad_branch2, w_down)
    d_hidden_in = gelu_back(d_hidden)[0].astype(jnp.bfloat16)
    d_up = inner_rows(act2, d_hidden_in)
    d_up_bias = jnp.sum(d_hidden_in.astype(jnp.float32), axis=0)
    d_act2 = times_transpose(d_hidden_in, w_up)
    d_mid_norm, d_gain2, d_shift2 = ln2_back(d_act2)
    mlp_owned = (
        lax.psum_scatter(d_gain2, "fsdp", scatter_dimension=0, tiled=True),
        lax.psum_scatter(d_shift2, "fsdp", scatter_dimension=0, tiled=True),
        lax.psum_scatter(d_up, "fsdp", scatter_dimension=0, tiled=True),
        lax.psum_scatter(d_up_bias, "fsdp", scatter_dimension=0, tiled=True),
        lax.psum_scatter(d_down, "fsdp", scatter_dimension=0, tiled=True),
        lax.psum_scatter(d_down_bias, "fsdp", scatter_dimension=0, tiled=True),
    )
    mlp_total = lax.psum(
        (mlp_owned[0], mlp_owned[1], mlp_owned[2], mlp_owned[3], mlp_owned[4], mlp_owned[5]), "ctx"
    )
    d_mid = grad_out + d_mid_norm
    grad_branch1 = d_mid.astype(jnp.bfloat16)
    d_out = inner_rows(attn, grad_branch1)
    d_out_bias = jnp.sum(grad_branch1.astype(jnp.float32), axis=0)
    d_attn = times_transpose(grad_branch1, w_out).reshape(rows, heads, HEAD_DIM)
    scaled = (d_attn / totals_rows[:, :, None]).astype(jnp.bfloat16)
    correction = jnp.sum(d_attn * attended, axis=2) / totals_rows
    zero_rows = jnp.zeros((rows, heads, HEAD_DIM), jnp.float32)

    def back_step(d_query, parts):
        key_part, value_part, part_place = parts
        exponent, d_raw = score_grads(
            query3, scaled, correction, query_place, key_part, value_part, part_place
        )
        d_query = d_query + jnp.einsum(
            "hqk,khd->qhd", d_raw, key_part, preferred_element_type=jnp.float32
        )
        d_key = jnp.einsum("hqk,qhd->khd", d_raw, query3, preferred_element_type=jnp.float32)
        d_value = jnp.einsum(
            "hqk,qhd->khd",
            exponent.astype(jnp.bfloat16),
            scaled,
            preferred_element_type=jnp.float32,
        )
        return (d_query, (d_key, d_value))

    d_query, (key_terms, value_terms) = lax.scan(
        back_step, zero_rows, (key_blocks, value_blocks, place_blocks)
    )
    d_keys, d_values = (
        lax.psum_scatter(key_terms.reshape(-1, width), "ctx", scatter_dimension=0, tiled=True),
        lax.psum_scatter(value_terms.reshape(-1, width), "ctx", scatter_dimension=0, tiled=True),
    )
    grad_query = d_query.reshape(rows, width).astype(jnp.bfloat16)
    grad_keys = d_keys.astype(jnp.bfloat16)
    grad_values = d_values.astype(jnp.bfloat16)
    grad_qkv = jnp.concatenate([grad_query, grad_keys, grad_values], axis=1)
    d_qkv = inner_rows(act1, grad_qkv)
    d_qv_bias = jnp.concatenate(
        [
            jnp.sum(grad_query.astype(jnp.float32), axis=0),
            jnp.sum(grad_values.astype(jnp.float32), axis=0),
        ]
    )
    d_act1 = times_transpose(grad_qkv, w_qkv)
    d_input_norm, d_gain1, d_shift1 = ln1_back(d_act1)
    input_grad = d_mid + d_input_norm
    attn_owned = (
        lax.psum_scatter(d_gain1, "fsdp", scatter_dimension=0, tiled=True),
        lax.psum_scatter(d_shift1, "fsdp", scatter_dimension=0, tiled=True),
        lax.psum_scatter(d_qkv, "fsdp", scatter_dimension=0, tiled=True),
        lax.psum_scatter(d_qv_bias, "fsdp", scatter_dimension=0, tiled=True),
        lax.psum_scatter(d_out, "fsdp", scatter_dimension=0, tiled=True),
        lax.psum_scatter(d_out_bias, "fsdp", scatter_dimension=0, tiled=True),
    )
    attn_total = lax.psum(
        (attn_owned[0], attn_owned[1], attn_owned[2], attn_owned[3], attn_owned[4], attn_owned[5]),
        "ctx",
    )
    return (
        result[None],
        input_grad[None],
        attn_total[0],
        attn_total[1],
        attn_total[2],
        attn_total[3],
        attn_total[4],
        attn_total[5],
        mlp_total[0],
        mlp_total[1],
        mlp_total[2],
        mlp_total[3],
        mlp_total[4],
        mlp_total[5],
    )


def solution(mesh):
    return jax.shard_map(
        on_device,
        mesh=mesh,
        in_specs=(
            P("fsdp", "ctx", None),
            P("fsdp"),
            P("fsdp"),
            P("fsdp", None),
            P("fsdp"),
            P("fsdp", None),
            P("fsdp"),
            P("fsdp"),
            P("fsdp"),
            P("fsdp", None),
            P("fsdp"),
            P("fsdp", None),
            P("fsdp"),
            P(),
            P("fsdp", "ctx", None),
        ),
        out_specs=(
            P("fsdp", "ctx", None),
            P("fsdp", "ctx", None),
            P("fsdp"),
            P("fsdp"),
            P("fsdp", None),
            P("fsdp"),
            P("fsdp", None),
            P("fsdp"),
            P("fsdp"),
            P("fsdp"),
            P("fsdp", None),
            P("fsdp"),
            P("fsdp", None),
            P("fsdp"),
        ),
        check_vma=False,
    )
```

profile of v0, /device:TPU:0, one launch (start us, length us, event | category | flops | bytes accessed | tf_op | source)
XLA Modules:
  0.0 3008.3 jit_solution(12149930245180257995)
XLA Ops:
  27.1 84.4 %all-gather.7.cloned.1.call-done = bf16[1600,4800]{1,0:T(8,128)(2,1)} async-done(((bf16[400,4800]{1,0:T(8,128)(2,1)}), bf16[1600,4800]{1,0:T(8,128)(2,1)}) %all-gather.7.cloned.1.call-update) | async-done | bytes 15360016 | tf_op jit(solution)/shard_map/all_gather | solution.py:86
  129.7 59.7 %all-gather.11.cloned.1.call-done = bf16[1024,1600]{0,1:T(8,128)(2,1)} async-done(((bf16[128,1600]{0,1:T(8,128)(2,1)}), bf16[1024,1600]{0,1:T(8,128)(2,1)}) %all-gather.11.cloned.1.call-update) | async-done | bytes 3276816 | tf_op jit(solution)/shard_map/all_gather | solution.py:106
  202.3 52.1 %all-gather.9.cloned.1.call-done = bf16[1024,1600]{0,1:T(8,128)(2,1)} async-done(((bf16[128,1600]{0,1:T(8,128)(2,1)}), bf16[1024,1600]{0,1:T(8,128)(2,1)}) %all-gather.9.cloned.1.call-update) | async-done | bytes 3276816 | tf_op jit(solution)/shard_map/all_gather | solution.py:105
  280.8 14.0 all-gather.13.cloned.1.call-done
  299.9 125.3 %all-gather.15.cloned.1.call-done = bf16[1600,6400]{1,0:T(8,128)(2,1)} async-done(((bf16[400,6400]{1,0:T(8,128)(2,1)}), bf16[1600,6400]{1,0:T(8,128)(2,1)}) %all-gather.15.cloned.1.call-update) | async-done | bytes 20480016 | tf_op jit(solution)/shard_map/all_gather | solution.py:134
  437.4 122.6 %all-gather.17.cloned.1.call-done = bf16[6400,1600]{1,0:T(8,128)(2,1)} async-done(((bf16[1600,1600]{1,0:T(8,128)(2,1)}), bf16[6400,1600]{1,0:T(8,128)(2,1)}) %all-gather.17.cloned.1.call-update) | async-done | bytes 20480016 | tf_op jit(solution)/shard_map/all_gather | solution.py:136
  588.6 281.8 %while.29 = (s32[]{:T(128)}, f32[128,25,64]{0,2,1:T(8,128)}, f32[2,512,25,64]{1,0,3,2:T(2,128)}, f32[2,512,25,64]{1,0,3,2:T(2,128)}, bf16[2,512,25,64]{1,3,2,0:T...) while((s32[]{:T(128)}, f32[128,25,64]{0,2,1:T(8,128)}, ...), condition=%wide.region_12.13_spmd.clone, body=%wide.region_11.12_spmd.clone.sunk | while | flops 1063796736 | bytes 77221088 | solution.py:198
  611.8 59.0 %dynamic_update_slice.11 = f32[2,512,25,64]{1,0,3,2:T(2,128)} dynamic-update-slice(f32[2,512,25,64]{1,0,3,2:T(2,128)} %get-tuple-element.526, f32[1,512,25,64]{1,0,3,2:T(1,128)} %copy.101, s32[]{:T(128)S(6)} %copy.126, s32[]{:T(128)} %constant.73.clone.1..sunk.1, s32[]{:T(128)} %constant.73.clone.1..sunk.1, s32[]{:T(128)} %constant.73.clone.1..sunk.1) | dynamic-update-slice | bytes 6553604 | tf_op jit(solution)/shard_map/while/body/jit(dynamic_update_index_in_dim)/dynamic_update_slice | solution.py:198
  670.8 58.8 %dynamic_update_slice.12 = f32[2,512,25,64]{1,0,3,2:T(2,128)} dynamic-update-slice(f32[2,512,25,64]{1,0,3,2:T(2,128)} %get-tuple-element.527, f32[1,512,25,64]{1,0,3,2:T(1,128)S(1)} %copy.102, s32[]{:T(128)S(6)} %copy.126, s32[]{:T(128)} %constant.73.clone.1..sunk.1, s32[]{:T(128)} %constant.73.clone.1..sunk.1, s32[]{:T(128)} %constant.73.clone.1..sunk.1) | dynamic-update-slice | bytes 6553604 | tf_op jit(solution)/shard_map/while/body/jit(dynamic_update_index_in_dim)/dynamic_update_slice | solution.py:198
  752.4 59.0 %dynamic_update_slice.11 = f32[2,512,25,64]{1,0,3,2:T(2,128)} dynamic-update-slice(f32[2,512,25,64]{1,0,3,2:T(2,128)} %get-tuple-element.526, f32[1,512,25,64]{1,0,3,2:T(1,128)} %copy.101, s32[]{:T(128)S(6)} %copy.126, s32[]{:T(128)} %constant.73.clone.1..sunk.1, s32[]{:T(128)} %constant.73.clone.1..sunk.1, s32[]{:T(128)} %constant.73.clone.1..sunk.1) | dynamic-update-slice | bytes 6553604 | tf_op jit(solution)/shard_map/while/body/jit(dynamic_update_index_in_dim)/dynamic_update_slice | solution.py:198
  811.4 58.8 %dynamic_update_slice.12 = f32[2,512,25,64]{1,0,3,2:T(2,128)} dynamic-update-slice(f32[2,512,25,64]{1,0,3,2:T(2,128)} %get-tuple-element.527, f32[1,512,25,64]{1,0,3,2:T(1,128)S(1)} %copy.102, s32[]{:T(128)S(6)} %copy.126, s32[]{:T(128)} %constant.73.clone.1..sunk.1, s32[]{:T(128)} %constant.73.clone.1..sunk.1, s32[]{:T(128)} %constant.73.clone.1..sunk.1) | dynamic-update-slice | bytes 6553604 | tf_op jit(solution)/shard_map/while/body/jit(dynamic_update_index_in_dim)/dynamic_update_slice | solution.py:198
  893.2 106.7 %reduce-scatter.7.cloned.1.call-done = f32[128,1600]{0,1:T(8,128)} async-done(((f32[1024,1600]{0,1:T(8,128)}), f32[128,1600]{0,1:T(8,128)}) %reduce-scatter.7.cloned.1.call-update) | async-done | bytes 819216 | tf_op jit(solution)/shard_map/reduce_scatter | solution.py:202
  1001.1 124.4 %reduce-scatter.9.cloned.1.call-done = f32[128,1600]{0,1:T(8,128)} async-done(((f32[1024,1600]{0,1:T(8,128)}), f32[128,1600]{0,1:T(8,128)}) %reduce-scatter.9.cloned.1.call-update) | async-done | bytes 819216 | tf_op jit(solution)/shard_map/reduce_scatter | solution.py:203
  1127.0 17.7 fusion.81
  1146.5 17.3 fusion.100
  1164.7 18.8 fusion.83
  1197.7 15.6 reduce-scatter.13.cloned.1.call-done
  1213.4 224.2 %reduce-scatter.11.cloned.1.call-done = f32[400,4800]{1,0:T(8,128)} async-done(((f32[1600,4800]{1,0:T(8,128)}), f32[400,4800]{1,0:T(8,128)}) %reduce-scatter.11.cloned.1.call-update) | async-done | bytes 7680016 | tf_op jit(solution)/shard_map/reduce_scatter | solution.py:222
  1437.5 295.6 %reduce-scatter.15.cloned.1.call-done = f32[400,6400]{1,0:T(8,128)} async-done(((f32[1600,6400]{1,0:T(8,128)}), f32[400,6400]{1,0:T(8,128)}) %reduce-scatter.15.cloned.1.call-update) | async-done | bytes 10240016 | tf_op jit(solution)/shard_map/reduce_scatter | solution.py:164
  1733.2 289.2 %reduce-scatter.17.cloned.1.call-done = f32[1600,1600]{1,0:T(8,128)} async-done(((f32[6400,1600]{1,0:T(8,128)}), f32[1600,1600]{1,0:T(8,128)}) %reduce-scatter.17.cloned.1.call-update) | async-done | bytes 10240016 | tf_op jit(solution)/shard_map/reduce_scatter | solution.py:166
  2024.3 14.6 fusion.65
  2038.9 19.7 all-reduce.25.cloned.1.call-done
  2064.9 39.9 %all-reduce.16 = (f32[400]{0:T(512)}, f32[400]{0:T(512)}, f32[800]{0:T(1024)}, f32[400]{0:T(512)}, f32[400]{0:T(512)}, /*index=5*/f32[400]{0:T(512)}, f32[1600]{0:T(1024)}, f32[400]{0:T(512)}) all-reduce(f32[400]{0:T(512)S(1)} %dynamic-slice.9, f32[400]{0:T(512)S(1)} %dynamic-slice.11, ...), channel_id=1, replica_groups=mesh['ctx'=8,'fsdp'=4] {'ctx'}, use_global_device_ids=true, to_apply=%region_19.20 | all-reduce | flops 4800 | bytes 38400 | tf_op jit(solution)/shard_map/psum | solution.py:227
  2104.8 874.7 %all-reduce.23.cloned.1.call-done = (f32[400,4800]{1,0:T(8,128)}, f32[400,1600]{1,0:T(8,128)}, f32[400,6400]{1,0:T(8,128)}, f32[1600,1600]{1,0:T(8,128)}) async-done(((f32[400,4800]{1,0:T(8,128)}, f32[400,1600]{1,0:T(8,128)}, f32[400,6400]{1,0:T(8,128)}, f32[1600,1600]{1,0:T(8,128)}), (f32[400,4800]{1,0:T(8,128)}, f32[400,1600]{1,0:T(8,128)}, f32[400,6400]{1,0:T(8,128)}, ...) | async-done | bytes 30720016 | tf_op jit(solution)/shard_map/psum | solution.py:227
  (262 shorter events, 249.5 us)
Async XLA Ops:
  7.3 104.1 %all-gather.7.cloned.1.call-start = ((), (), s32[]{:S(2)}) async-start(), calls=%async_computation.6 | async-start | bytes 19456000 | tf_op jit(solution)/shard_map/all_gather | solution.py:86
  8.0 181.3 %all-gather.11.cloned.1.call-start = ((), (), s32[]{:S(2)}) async-start(), calls=%async_computation.8 | async-start | bytes 3686400 | tf_op jit(solution)/shard_map/all_gather | solution.py:106
  26.5 95.6 %copy-start.23 = (f32[1600]{0:T(1024)}, f32[1600]{0:T(1024)S(1)}, u32[]{:S(2)}) copy-start(f32[1600]{0:T(1024)S(1)} %convert_element_type.103) | copy-start | bytes 19204
  124.9 129.4 %all-gather.9.cloned.1.call-start = ((), (), s32[]{:S(2)}) async-start(), calls=%async_computation.7 | async-start | bytes 3686400 | tf_op jit(solution)/shard_map/all_gather | solution.py:105
  126.9 167.9 %all-gather.13.cloned.1.call-start = ((), (), s32[]{:S(2)}) async-start(), calls=%async_computation.9 | async-start | bytes 6656000 | tf_op jit(solution)/shard_map/all_gather | solution.py:88
  127.5 297.6 %all-gather.15.cloned.1.call-start = ((), (), s32[]{:S(2)}) async-start(), calls=%async_computation.10 | async-start | bytes 25600000 | tf_op jit(solution)/shard_map/all_gather | solution.py:134
  128.1 431.9 %all-gather.17.cloned.1.call-start = ((), (), s32[]{:S(2)}) async-start(), calls=%async_computation.11 | async-start | bytes 26624000 | tf_op jit(solution)/shard_map/all_gather | solution.py:136
  128.7 871.2 %reduce-scatter.7.cloned.1.call-start = ((), (), s32[]{:S(2)}) async-start(), calls=%async_computation.12 | async-start | bytes 7372800 | tf_op jit(solution)/shard_map/reduce_scatter | solution.py:202
  129.4 295.7 %copy-start.27 = (f32[1600]{0:T(1024)}, f32[1600]{0:T(1024)S(1)}, u32[]{:S(2)}) copy-start(f32[1600]{0:T(1024)S(1)} %convert_element_type.113) | copy-start | bytes 19204
  299.6 285.1 %copy-start = (f32[128,1600]{0,1:T(8,128)}, f32[128,1600]{0,1:T(8,128)S(1)}, u32[]{:S(2)}) copy-start(f32[128,1600]{0,1:T(8,128)S(1)} %get-tuple-element.354) | copy-start | bytes 2457604
  299.9 260.2 %copy-start.14 = (bf16[1,128,1600]{1,2,0:T(8,128)(2,1)S(1)}, bf16[1,128,1600]{1,2,0:T(8,128)(2,1)}, u32[]{:S(2)}) copy-start(bf16[1,128,1600]{1,2,0:T(8,128)(2,1)} %param.33) | copy-start | bytes 1228804
  877.6 247.9 %reduce-scatter.9.cloned.1.call-start = ((), (), s32[]{:S(2)}) async-start(), calls=%async_computation.13 | async-start | bytes 7372800 | tf_op jit(solution)/shard_map/reduce_scatter | solution.py:203
  885.0 328.4 %reduce-scatter.13.cloned.1.call-start = ((), (), s32[]{:S(2)}) async-start(), calls=%async_computation.15 | async-start | bytes 13312000 | tf_op jit(solution)/shard_map/reduce_scatter | solution.py:224
  891.8 235.1 %copy-start.6 = (bf16[1,128,1600]{1,2,0:T(8,128)(2,1)S(1)}, bf16[1,128,1600]{1,2,0:T(8,128)(2,1)}, u32[]{:S(2)}) copy-start(bf16[1,128,1600]{1,2,0:T(8,128)(2,1)} %param.19) | copy-start | bytes 1228804
  891.8 235.1 %copy-start.24 = (f32[1600]{0:T(1024)S(1)}, f32[1600]{0:T(1024)}, u32[]{:S(2)}) copy-start(f32[1600]{0:T(1024)} %copy-done.23) | copy-start | bytes 19204
  891.8 235.1 %copy-start.26 = (f32[1600]{0:T(1024)S(1)}, f32[1600]{0:T(1024)}, u32[]{:S(2)}) copy-start(f32[1600]{0:T(1024)} %copy-done.25) | copy-start | bytes 19204
  891.8 235.1 %copy-start.30 = (f32[128]{0:T(128)S(1)}, f32[128]{0:T(128)}, u32[]{:S(2)}) copy-start(f32[128]{0:T(128)} %copy-done.29) | copy-start | bytes 1540
  891.9 235.1 %copy-start.32 = (f32[128]{0:T(128)S(1)}, f32[128]{0:T(128)}, u32[]{:S(2)}) copy-start(f32[128]{0:T(128)} %copy-done.31) | copy-start | bytes 1540
  891.9 545.7 %reduce-scatter.11.cloned.1.call-start = ((), (), s32[]{:S(2)}) async-start(), calls=%async_computation.14 | async-start | bytes 38912000 | tf_op jit(solution)/shard_map/reduce_scatter | solution.py:222
  1001.1 143.6 %copy-start.19 = (bf16[128,1600]{0,1:T(8,128)(2,1)}, bf16[128,1600]{0,1:T(8,128)(2,1)S(1)}, u32[]{:S(2)}) copy-start(bf16[128,1600]{0,1:T(8,128)(2,1)S(1)} %convert_element_type.124) | copy-start | bytes 1228804
  1144.7 588.4 %reduce-scatter.15.cloned.1.call-start = ((), (), s32[]{:S(2)}) async-start(), calls=%async_computation.16 | async-start | bytes 51200000 | tf_op jit(solution)/shard_map/reduce_scatter | solution.py:164
  1163.8 858.6 %reduce-scatter.17.cloned.1.call-start = ((), (), s32[]{:S(2)}) async-start(), calls=%async_computation.17 | async-start | bytes 53248000 | tf_op jit(solution)/shard_map/reduce_scatter | solution.py:166
  1183.6 875.1 %all-reduce.25.cloned.1.call-start = ((), (), s32[]{:S(2)}) async-start(), calls=%async_computation.19 | async-start | bytes 188416
  1197.7 1781.8 %all-reduce.23.cloned.1.call-start = ((), (), s32[]{:S(2)}) async-start(), calls=%async_computation.18 | async-start | bytes 62668800 | tf_op jit(solution)/shard_map/psum | solution.py:227
  (45 other events, 615.7 us)
Sparse Core Ops, SparseCore 0:
  9.7 101.7 all-gather.6
  125.0 64.2 all-gather.10
  192.0 62.3 all-gather.8
  255.7 39.0 all-gather.12
  296.3 128.8 all-gather.14
  426.6 133.3 all-gather.16
  877.7 122.1 reduce-scatter.6
  1004.1 121.3 reduce-scatter.8
  1128.7 84.6 reduce-scatter.12
  1215.9 221.6 reduce-scatter.10
  1440.2 292.9 reduce-scatter.14
  1735.6 286.6 reduce-scatter.16
  2026.3 32.3 all-reduce.24
  2063.4 916.0 all-reduce.22
where the time goes:
time: 3030 us; the launch traced here: 3010 us
  waiting for transfers between devices  2410 us (80%)
  local copies, waits for them, and re-layouts  333 us (11%)
  matrix products  178 us (6%)
  blocking collectives  53.7 us (2%)
    psum x1, waiting for transfers between devices, on_device(): lax.psum((attn_owned[0], attn_owned[1], attn_owned[2], attn_owned[3], att...  875 us
    reduce_scatter x1, waiting for transfers between devices, on_device(): lax.psum_scatter(d_up, 'fsdp', scatter_dimension=0, tiled=True)  296 us
    reduce_scatter x1, waiting for transfers between devices, on_device(): lax.psum_scatter(d_down, 'fsdp', scatter_dimension=0, tiled=True)  289 us
    dynamic_update_slice x8, local copies, waits for them, and re-layouts, on_device(): lax.scan(back_step, zero_rows, (key_blocks, value_blocks, place_blocks))  253 us
    reduce_scatter x1, waiting for transfers between devices, on_device(): lax.psum_scatter(d_qkv, 'fsdp', scatter_dimension=0, tiled=True)  224 us
    all_gather x1, waiting for transfers between devices, on_device(): lax.all_gather(up_weight, 'fsdp', axis=0, tiled=True)  125 us
    reduce_scatter x1, waiting for transfers between devices, on_device(): lax.psum_scatter(value_terms.reshape(-1, width), 'ctx', scatter_dimension...  124 us
    all_gather x1, waiting for transfers between devices, on_device(): lax.all_gather(down_weight, 'fsdp', axis=0, tiled=True)  123 us
  transfers between devices with their start and end apart: 14, of which 14 were waited for; matrix products, arithmetic and copies ran while one was open for 6% of the time, Pallas kernels for 0%

commit v1 on v0

--- a/solution.py
+++ b/solution.py
@@ -6,6 +6,17 @@
 HEAD_DIM = 64
 EPS = 1e-05
 SCALE = 0.125
+
+
+def collect(x, axis, dim):
+    ways = lax.axis_size(axis)
+    pieces = [x]
+    for far in range(1, ways):
+        pieces.append(
+            lax.ppermute(pieces[far - 1], axis, [(d, (d - 1) % ways) for d in range(ways)])
+        )
+    line = jnp.concatenate(pieces, axis=dim)
+    return jnp.roll(line, lax.axis_index(axis) * x.shape[dim], axis=dim)
 
 
 def layer_norm(value, gain, shift):
@@ -83,7 +94,7 @@
     attn_parts = (
         lax.all_gather(ln1_gain, "fsdp", axis=0, tiled=True),
         lax.all_gather(ln1_shift, "fsdp", axis=0, tiled=True),
-        lax.all_gather(qkv_weight, "fsdp", axis=0, tiled=True),
+        collect(qkv_weight, "fsdp", 0),
         lax.all_gather(qv_bias, "fsdp", axis=0, tiled=True),
         lax.all_gather(out_weight, "fsdp", axis=0, tiled=True),
         lax.all_gather(out_bias, "fsdp", axis=0, tiled=True),

time: 3030 us -> 3110 us (1.026)
  local copies, waits for them, and re-layouts: 333 us -> 365 us
    ppermute x0 -> x3, waiting for transfers between devices: none -> 85.9 us  [collect(): lax.ppermute(pieces[far - 1], axis, [(d, (d - 1) % ways) for d in range(w...]
    all_gather x1 -> x0, waiting for transfers between devices: 84.4 us -> none  [on_device(): lax.all_gather(qkv_weight, 'fsdp', axis=0, tiled=True)]
    unnamed x136 -> x131, local copies, waits for them, and re-layouts: 61.4 us -> 93.2 us
  transfers between devices with their start and end apart: 14 -> 16, of which waited for: 14 -> 15; matrix products, arithmetic and copies ran while one was open for 6% -> 6% of each run, Pallas kernels for 0% -> 0%
where the time goes in v1:
time: 3110 us; the launch traced here: 3080 us
  waiting for transfers between devices  2400 us (77%)
  local copies, waits for them, and re-layouts  365 us (12%)
  matrix products  195 us (6%)
  blocking collectives  81.4 us (3%)
    psum x1, waiting for transfers between devices, on_device(): lax.psum((attn_owned[0], attn_owned[1], attn_owned[2], attn_owned[3], att...  875 us
    reduce_scatter x1, waiting for transfers between devices, on_device(): lax.psum_scatter(d_up, 'fsdp', scatter_dimension=0, tiled=True)  295 us
    reduce_scatter x1, waiting for transfers between devices, on_device(): lax.psum_scatter(d_down, 'fsdp', scatter_dimension=0, tiled=True)  289 us
    dynamic_update_slice x8, local copies, waits for them, and re-layouts, on_device(): lax.scan(back_step, zero_rows, (key_blocks, value_blocks, place_blocks))  249 us
    reduce_scatter x1, waiting for transfers between devices, on_device(): lax.psum_scatter(d_qkv, 'fsdp', scatter_dimension=0, tiled=True)  224 us
    all_gather x1, waiting for transfers between devices, on_device(): lax.all_gather(up_weight, 'fsdp', axis=0, tiled=True)  125 us
    reduce_scatter x1, waiting for transfers between devices, on_device(): lax.psum_scatter(value_terms.reshape(-1, width), 'ctx', scatter_dimension...  124 us
    all_gather x1, waiting for transfers between devices, on_device(): lax.all_gather(down_weight, 'fsdp', axis=0, tiled=True)  123 us
  transfers between devices with their start and end apart: 16, of which 15 were waited for; matrix products, arithmetic and copies ran while one was open for 6% of the time, Pallas kernels for 0%

profile of v1, /device:TPU:0, one launch (start us, length us, event | category | flops | bytes accessed | tf_op | source)
XLA Modules:
  0.0 3083.4 jit_solution(2622517077100259733)
XLA Ops:
  9.7 43.1 %collective-permute-done = bf16[400,4800]{1,0:T(8,128)(2,1)S(1)} collective-permute-done((bf16[400,4800]{1,0:T(8,128)(2,1)}, bf16[400,4800]{1,0:T(8,128)(2,1)S(1)}, u32[]{:S(2)}, u32[]{:S(2)}) %collective-permute-start) | collective-permute-done | bytes 3840032 | tf_op jit(solution)/shard_map/ppermute | solution.py:16
  56.5 42.8 %collective-permute-done.1 = bf16[400,4800]{1,0:T(8,128)(2,1)} collective-permute-done((bf16[400,4800]{1,0:T(8,128)(2,1)S(1)}, bf16[400,4800]{1,0:T(8,128)(2,1)}, u32[]{:S(2)}, u32[]{:S(2)}) %collective-permute-start.1) | collective-permute-done | bytes 3840032 | tf_op jit(solution)/shard_map/ppermute | solution.py:16
  111.6 41.3 %all-reduce.19 = (bf16[1600]{0:T(1024)(128)(2,1)S(1)}, bf16[1600]{0:T(1024)(128)(2,1)S(1)}, bf16[3200]{0:T(1024)(128)(2,1)S(1)}, bf16[1600]{0:T(1024)(128)(2,1)S...) all-reduce(bf16[1600]{0:T(1024)(128)(2,1)S(1)} %dynamic-update-slic, ...), channel_id=1, replica_groups=mesh['ctx'=8,'fsdp'=4] {'fsdp'}, use_global_device_ids=true, to_apply=%add.1 | all-reduce | flops 19200 | bytes 76800
  202.8 58.8 %all-gather.6.cloned.1.call-done = bf16[1024,1600]{0,1:T(8,128)(2,1)} async-done(((bf16[128,1600]{0,1:T(8,128)(2,1)}), bf16[1024,1600]{0,1:T(8,128)(2,1)}) %all-gather.6.cloned.1.call-update) | async-done | bytes 3276816 | tf_op jit(solution)/shard_map/all_gather | solution.py:116
  274.5 51.5 %all-gather.8.cloned.1.call-done = bf16[1024,1600]{0,1:T(8,128)(2,1)} async-done(((bf16[128,1600]{0,1:T(8,128)(2,1)}), bf16[1024,1600]{0,1:T(8,128)(2,1)}) %all-gather.8.cloned.1.call-update) | async-done | bytes 3276816 | tf_op jit(solution)/shard_map/all_gather | solution.py:117
  339.6 22.3 while.28
  371.7 125.3 %all-gather.12.cloned.1.call-done = bf16[1600,6400]{1,0:T(8,128)(2,1)} async-done(((bf16[400,6400]{1,0:T(8,128)(2,1)}), bf16[1600,6400]{1,0:T(8,128)(2,1)}) %all-gather.12.cloned.1.call-update) | async-done | bytes 20480016 | tf_op jit(solution)/shard_map/all_gather | solution.py:145
  509.3 122.6 %all-gather.14.cloned.1.call-done = bf16[6400,1600]{1,0:T(8,128)(2,1)} async-done(((bf16[1600,1600]{1,0:T(8,128)(2,1)}), bf16[6400,1600]{1,0:T(8,128)(2,1)}) %all-gather.14.cloned.1.call-update) | async-done | bytes 20480016 | tf_op jit(solution)/shard_map/all_gather | solution.py:147
  660.6 284.8 %while.29 = (s32[]{:T(128)}, f32[128,25,64]{0,2,1:T(8,128)}, f32[2,512,25,64]{1,0,3,2:T(2,128)}, f32[2,512,25,64]{1,0,3,2:T(2,128)}, bf16[2,512,25,64]{1,3,2,0:T...) while((s32[]{:T(128)}, f32[128,25,64]{0,2,1:T(8,128)}, ...), condition=%wide.region_12.13_spmd.clone, body=%wide.region_11.12_spmd.clone.sunk | while | flops 1063796736 | bytes 98520288 | solution.py:209
  677.8 58.8 %dynamic_update_slice.11 = f32[2,512,25,64]{1,0,3,2:T(2,128)} dynamic-update-slice(f32[2,512,25,64]{1,0,3,2:T(2,128)} %get-tuple-element.526, f32[1,512,25,64]{1,0,3,2:T(1,128)S(1)} %copy.101, s32[]{:T(128)S(6)} %copy.133, s32[]{:T(128)} %constant.92.clone.1..sunk.1, s32[]{:T(128)} %constant.92.clone.1..sunk.1, s32[]{:T(128)} %constant.92.clone.1..sunk.1) | dynamic-update-slice | bytes 6553604 | tf_op jit(solution)/shard_map/while/body/jit(dynamic_update_index_in_dim)/dynamic_update_slice | solution.py:209
  744.2 58.8 %dynamic_update_slice.12 = f32[2,512,25,64]{1,0,3,2:T(2,128)} dynamic-update-slice(f32[2,512,25,64]{1,0,3,2:T(2,128)} %get-tuple-element.527, f32[1,512,25,64]{1,0,3,2:T(1,128)S(1)} %copy.102, s32[]{:T(128)S(6)} %copy.133, s32[]{:T(128)} %constant.92.clone.1..sunk.1, s32[]{:T(128)} %constant.92.clone.1..sunk.1, s32[]{:T(128)} %constant.92.clone.1..sunk.1) | dynamic-update-slice | bytes 6553604 | tf_op jit(solution)/shard_map/while/body/jit(dynamic_update_index_in_dim)/dynamic_update_slice | solution.py:209
  820.0 58.8 %dynamic_update_slice.11 = f32[2,512,25,64]{1,0,3,2:T(2,128)} dynamic-update-slice(f32[2,512,25,64]{1,0,3,2:T(2,128)} %get-tuple-element.526, f32[1,512,25,64]{1,0,3,2:T(1,128)S(1)} %copy.101, s32[]{:T(128)S(6)} %copy.133, s32[]{:T(128)} %constant.92.clone.1..sunk.1, s32[]{:T(128)} %constant.92.clone.1..sunk.1, s32[]{:T(128)} %constant.92.clone.1..sunk.1) | dynamic-update-slice | bytes 6553604 | tf_op jit(solution)/shard_map/while/body/jit(dynamic_update_index_in_dim)/dynamic_update_slice | solution.py:209
  886.4 58.8 %dynamic_update_slice.12 = f32[2,512,25,64]{1,0,3,2:T(2,128)} dynamic-update-slice(f32[2,512,25,64]{1,0,3,2:T(2,128)} %get-tuple-element.527, f32[1,512,25,64]{1,0,3,2:T(1,128)S(1)} %copy.102, s32[]{:T(128)S(6)} %copy.133, s32[]{:T(128)} %constant.92.clone.1..sunk.1, s32[]{:T(128)} %constant.92.clone.1..sunk.1, s32[]{:T(128)} %constant.92.clone.1..sunk.1) | dynamic-update-slice | bytes 6553604 | tf_op jit(solution)/shard_map/while/body/jit(dynamic_update_index_in_dim)/dynamic_update_slice | solution.py:209
  968.3 106.7 %reduce-scatter.7.cloned.1.call-done = f32[128,1600]{0,1:T(8,128)} async-done(((f32[1024,1600]{0,1:T(8,128)}), f32[128,1600]{0,1:T(8,128)}) %reduce-scatter.7.cloned.1.call-update) | async-done | bytes 819216 | tf_op jit(solution)/shard_map/reduce_scatter | solution.py:213
  1076.2 124.4 %reduce-scatter.9.cloned.1.call-done = f32[128,1600]{0,1:T(8,128)} async-done(((f32[1024,1600]{0,1:T(8,128)}), f32[128,1600]{0,1:T(8,128)}) %reduce-scatter.9.cloned.1.call-update) | async-done | bytes 819216 | tf_op jit(solution)/shard_map/reduce_scatter | solution.py:214
  1202.1 17.7 fusion.85
  1221.5 17.3 fusion.104
  1239.8 18.8 fusion.86
  1288.5 224.3 %reduce-scatter.11.cloned.1.call-done = f32[400,4800]{1,0:T(8,128)} async-done(((f32[1600,4800]{1,0:T(8,128)}), f32[400,4800]{1,0:T(8,128)}) %reduce-scatter.11.cloned.1.call-update) | async-done | bytes 7680016 | tf_op jit(solution)/shard_map/reduce_scatter | solution.py:233
  1512.8 295.5 %reduce-scatter.15.cloned.1.call-done = f32[400,6400]{1,0:T(8,128)} async-done(((f32[1600,6400]{1,0:T(8,128)}), f32[400,6400]{1,0:T(8,128)}) %reduce-scatter.15.cloned.1.call-update) | async-done | bytes 10240016 | tf_op jit(solution)/shard_map/reduce_scatter | solution.py:175
  1808.3 289.3 %reduce-scatter.17.cloned.1.call-done = f32[1600,1600]{1,0:T(8,128)} async-done(((f32[6400,1600]{1,0:T(8,128)}), f32[1600,1600]{1,0:T(8,128)}) %reduce-scatter.17.cloned.1.call-update) | async-done | bytes 10240016 | tf_op jit(solution)/shard_map/reduce_scatter | solution.py:177
  2114.8 18.9 all-reduce.25.cloned.1.call-done
  2139.9 40.1 %all-reduce.16 = (f32[400]{0:T(512)}, f32[400]{0:T(512)}, f32[800]{0:T(1024)}, f32[400]{0:T(512)}, f32[400]{0:T(512)}, /*index=5*/f32[400]{0:T(512)}, f32[1600]{0:T(1024)}, f32[400]{0:T(512)}) all-reduce(f32[400]{0:T(512)S(1)} %dynamic-slice.9, f32[400]{0:T(512)S(1)} %dynamic-slice.11, ...), channel_id=1, replica_groups=mesh['ctx'=8,'fsdp'=4] {'ctx'}, use_global_device_ids=true, to_apply=%region_19.20 | all-reduce | flops 4800 | bytes 38400 | tf_op jit(solution)/shard_map/psum | solution.py:238
  2180.0 874.7 %all-reduce.23.cloned.1.call-done = (f32[400,4800]{1,0:T(8,128)}, f32[400,1600]{1,0:T(8,128)}, f32[400,6400]{1,0:T(8,128)}, f32[1600,1600]{1,0:T(8,128)}) async-done(((f32[400,4800]{1,0:T(8,128)}, f32[400,1600]{1,0:T(8,128)}, f32[400,6400]{1,0:T(8,128)}, f32[1600,1600]{1,0:T(8,128)}), (f32[400,4800]{1,0:T(8,128)}, f32[400,1600]{1,0:T(8,128)}, f32[400,6400]{1,0:T(8,128)}, ...) | async-done | bytes 30720016 | tf_op jit(solution)/shard_map/psum | solution.py:238
  (261 shorter events, 315.7 us)
Async XLA Ops:
  7.2 254.4 %all-gather.6.cloned.1.call-start = ((), (), s32[]{:S(2)}) async-start(), calls=%async_computation.6 | async-start | bytes 3686400 | tf_op jit(solution)/shard_map/all_gather | solution.py:116
  7.2 45.6 %collective-permute-start = (bf16[400,4800]{1,0:T(8,128)(2,1)}, bf16[400,4800]{1,0:T(8,128)(2,1)S(1)}, u32[]{:S(2)}, u32[]{:S(2)}) collective-permute-start(bf16[400,4800]{1,0:T(8,128)(2,1)} %param.22), channel_id=1, source_target_pairs={{0,3},{1,0},{2,1},{3,2},{4,7},{5,4},{6,5},{7,6},{8,11},{9,8},{10,9... | collective-permute-start | bytes 11520008 | tf_op jit(solution)/shard_map/ppermute | solution.py:16
  54.7 44.6 %collective-permute-start.1 = (bf16[400,4800]{1,0:T(8,128)(2,1)S(1)}, bf16[400,4800]{1,0:T(8,128)(2,1)}, u32[]{:S(2)}, u32[]{:S(2)}) collective-permute-start(bf16[400,4800]{1,0:T(8,128)(2,1)S(1)} %collective-permute-done), channel_id=1, source_target_pairs={{0,3},{1,0},{2,1},{3,2},{4,7},{5,4},{6,5},{7,6},{8,11},{9,8},{10,9... | collective-permute-start | bytes 11520008 | tf_op jit(solution)/shard_map/ppermute | solution.py:16
  99.3 67.0 %collective-permute-start.2 = (bf16[400,4800]{1,0:T(8,128)(2,1)}, bf16[400,4800]{1,0:T(8,128)(2,1)}, u32[]{:S(2)}, u32[]{:S(2)}) collective-permute-start(bf16[400,4800]{1,0:T(8,128)(2,1)} %collective-permute-done.1), channel_id=1, source_target_pairs={{0,3},{1,0},{2,1},{3,2},{4,7},{5,4},{6,5},{7,6},{8,11},{9,8},{10,9... | collective-permute-start | bytes 11520008 | tf_op jit(solution)/shard_map/ppermute | solution.py:16
  197.0 129.1 %all-gather.8.cloned.1.call-start = ((), (), s32[]{:S(2)}) async-start(), calls=%async_computation.7 | async-start | bytes 3686400 | tf_op jit(solution)/shard_map/all_gather | solution.py:117
  199.9 166.8 %all-gather.10.cloned.1.call-start = ((), (), s32[]{:S(2)}) async-start(), calls=%async_computation.8 | async-start | bytes 6656000 | tf_op jit(solution)/shard_map/all_gather | solution.py:99
  200.6 296.4 %all-gather.12.cloned.1.call-start = ((), (), s32[]{:S(2)}) async-start(), calls=%async_computation.9 | async-start | bytes 25600000 | tf_op jit(solution)/shard_map/all_gather | solution.py:145
  201.2 430.7 %all-gather.14.cloned.1.call-start = ((), (), s32[]{:S(2)}) async-start(), calls=%async_computation.10 | async-start | bytes 26624000 | tf_op jit(solution)/shard_map/all_gather | solution.py:147
  201.8 873.1 %reduce-scatter.7.cloned.1.call-start = ((), (), s32[]{:S(2)}) async-start(), calls=%async_computation.11 | async-start | bytes 7372800 | tf_op jit(solution)/shard_map/reduce_scatter | solution.py:213
  202.6 294.5 %copy-start.30 = (f32[1600]{0:T(1024)}, f32[1600]{0:T(1024)S(1)}, u32[]{:S(2)}) copy-start(f32[1600]{0:T(1024)S(1)} %convert_element_type.113) | copy-start | bytes 19204
  371.5 285.2 %copy-start.1 = (f32[128,1600]{0,1:T(8,128)}, f32[128,1600]{0,1:T(8,128)S(1)}, u32[]{:S(2)}) copy-start(f32[128,1600]{0,1:T(8,128)S(1)} %get-tuple-element.354) | copy-start | bytes 2457604
  371.7 260.2 %copy-start.17 = (bf16[1,128,1600]{1,2,0:T(8,128)(2,1)S(1)}, bf16[1,128,1600]{1,2,0:T(8,128)(2,1)}, u32[]{:S(2)}) copy-start(bf16[1,128,1600]{1,2,0:T(8,128)(2,1)} %param.33) | copy-start | bytes 1228804
  952.7 247.9 %reduce-scatter.9.cloned.1.call-start = ((), (), s32[]{:S(2)}) async-start(), calls=%async_computation.12 | async-start | bytes 7372800 | tf_op jit(solution)/shard_map/reduce_scatter | solution.py:214
  960.0 328.5 %reduce-scatter.13.cloned.1.call-start = ((), (), s32[]{:S(2)}) async-start(), calls=%async_computation.14 | async-start | bytes 13312000 | tf_op jit(solution)/shard_map/reduce_scatter | solution.py:235
  966.8 235.2 %copy-start.5 = (bf16[1,128,1600]{1,2,0:T(8,128)(2,1)S(1)}, bf16[1,128,1600]{1,2,0:T(8,128)(2,1)}, u32[]{:S(2)}) copy-start(bf16[1,128,1600]{1,2,0:T(8,128)(2,1)} %param.19) | copy-start | bytes 1228804
  966.9 235.2 %copy-start.27 = (f32[1600]{0:T(1024)S(1)}, f32[1600]{0:T(1024)}, u32[]{:S(2)}) copy-start(f32[1600]{0:T(1024)} %copy-done.26) | copy-start | bytes 19204
  966.9 235.2 %copy-start.29 = (f32[1600]{0:T(1024)S(1)}, f32[1600]{0:T(1024)}, u32[]{:S(2)}) copy-start(f32[1600]{0:T(1024)} %copy-done.28) | copy-start | bytes 19204
  966.9 235.2 %copy-start.33 = (f32[128]{0:T(128)S(1)}, f32[128]{0:T(128)}, u32[]{:S(2)}) copy-start(f32[128]{0:T(128)} %copy-done.32) | copy-start | bytes 1540
  966.9 235.2 %copy-start.35 = (f32[128]{0:T(128)S(1)}, f32[128]{0:T(128)}, u32[]{:S(2)}) copy-start(f32[128]{0:T(128)} %copy-done.34) | copy-start | bytes 1540
  966.9 545.9 %reduce-scatter.11.cloned.1.call-start = ((), (), s32[]{:S(2)}) async-start(), calls=%async_computation.13 | async-start | bytes 38912000 | tf_op jit(solution)/shard_map/reduce_scatter | solution.py:233
  1219.8 588.5 %reduce-scatter.15.cloned.1.call-start = ((), (), s32[]{:S(2)}) async-start(), calls=%async_computation.15 | async-start | bytes 51200000 | tf_op jit(solution)/shard_map/reduce_scatter | solution.py:175
  1238.8 858.7 %reduce-scatter.17.cloned.1.call-start = ((), (), s32[]{:S(2)}) async-start(), calls=%async_computation.16 | async-start | bytes 53248000 | tf_op jit(solution)/shard_map/reduce_scatter | solution.py:177
  1258.7 875.1 %all-reduce.25.cloned.1.call-start = ((), (), s32[]{:S(2)}) async-start(), calls=%async_computation.18 | async-start | bytes 188416
  1272.9 1781.8 %all-reduce.23.cloned.1.call-start = ((), (), s32[]{:S(2)}) async-start(), calls=%async_computation.17 | async-start | bytes 62668800 | tf_op jit(solution)/shard_map/psum | solution.py:238
  (41 other events, 455.3 us)
Sparse Core Ops, SparseCore 0:
  197.1 64.4 all-gather.5
  263.7 62.3 all-gather.7
  327.6 39.0 all-gather.9
  368.1 128.8 all-gather.11
  498.4 133.3 all-gather.13
  952.8 122.1 reduce-scatter.6
  1079.2 121.3 reduce-scatter.8
  1203.8 84.6 reduce-scatter.12
  1291.1 221.6 reduce-scatter.10
  1515.2 292.9 reduce-scatter.14
  1810.9 286.6 reduce-scatter.16
  2101.4 32.2 all-reduce.24
  2138.6 915.9 all-reduce.22
